TPU v7x, 32 devices: a whole 2x2x4 slice. The times are simulated.
32 devices in a mesh: ctx: 4 (over z), grp: 8 (over y, x, core).
Axes of the slice: x: 2, y: 2, z: 4, core: 2. Of those that a mesh axis runs over, the one named last changes fastest.
Arguments:
- latent: bfloat16 [8, 512, 576], P('grp', 'ctx'), may hold values from -6 to 6
- queries: bfloat16 [8, 16, 73728], P('grp', 'ctx'), may hold values from -4 to 4
- out_grad: bfloat16 [8, 16, 65536], P('grp', 'ctx'), may hold values from -6 to 6
- hidden: bfloat16 [8, 512, 7168], P('grp', None, 'ctx'), may hold values from -6 to 6
- doc_ids: int32 [8, 512], P('grp', 'ctx'), may hold values from 0 to 7, never falling along the last dimension, each value on 1 to 256 neighbouring positions
- clip_limits: float32 [8, 8], P('grp'), may hold values from 0.05 to 20
Outputs:
- grad_keys: bfloat16 [8, 512, 576], P('grp', 'ctx')
- weight_grad: float32 [576, 7168], P('grp', 'ctx')
Inputs may be any that keep to these rules, and one draw needn't show every extreme that they name: `doc_ids`: within each group the ids never fall; each document has 1 to 256 tokens and one has exactly 256.
All inputs are finite; a program needn't handle non-finite values.
Results may differ from a plain program's by a relative error of at most 0.0095.
Values may be sent and summed in bfloat16 or wider, within the bound.
A program may use at most 64 MiB of HBM per device.

v0:
```python
import functools
import math

import jax
import jax.numpy as jnp
from jax import lax
from jax.experimental import pallas as pl
from jax.experimental.pallas import tpu as pltpu
from jax.sharding import PartitionSpec as P

LATENT = 512
HEADS = 128


score_scale = 192.0 ** (-0.5)
norm_eps = 1e-06

BF = jnp.bfloat16
F32 = jnp.float32


def dot(a, b, dims):
    return lax.dot_general(a, b, (dims, ((), ())), preferred_element_type=F32)


def col_chunks(cols):
    half = cols // 2
    first = -(-(half // 2) // 128) * 128
    out = []
    for start, width in ((0, first), (first, half - first)):
        for path in (0, 1):
            out.append((path * half + start, width, path))
    return out


def body(cfg, *refs):
    n = cfg["n"]
    tok = cfg["tok"]
    kw = cfg["kw"]
    qd = cfg["qd"]
    reach = cfg["reach"]
    rows_of = cfg["rows_of"]
    span = cfg["span"]
    ndocs = cfg["ndocs"]
    pieces = cfg["pieces"]
    scatter = cfg["scatter"]
    (lat_t, ids, lim, q_hbm, g_hbm, h_hbm, gk_out, w_out) = refs[:8]
    (qraw, graw, hid, qs, gs, kbuf, idbuf, psend, precv, full, scT, local_sem, key_s, key_r,
     id_s, id_r, part_s, part_r, up_s, up_r, dn_s, dn_r, lat) = refs[8:31]
    tail = refs[31:]
    d = lax.axis_index("ctx")
    m = lax.axis_index("grp")
    wide = -(-kw // 128) * 128
    pad = wide - kw
    pair = 2 * kw

    copy_q = pltpu.make_async_copy(q_hbm, qraw, local_sem.at[0])
    copy_g = pltpu.make_async_copy(g_hbm, graw, local_sem.at[1])
    copy_h = pltpu.make_async_copy(h_hbm, hid, local_sem.at[2])
    copy_q.start()
    copy_g.start()
    copy_h.start()

    def remote(src, dst, ss, rs, **where):
        axis, index = next(iter(where.items()))
        return pltpu.make_async_remote_copy(
            src_ref=src, dst_ref=dst, send_sem=ss, recv_sem=rs,
            device_id={axis: index}, device_id_type=pl.DeviceIdType.MESH,
        )

    barrier = pltpu.get_barrier_semaphore()
    for o in range(1, n):
        pl.semaphore_signal(barrier, inc=1, device_id={"ctx": lax.rem(d + o, n)},
                            device_id_type=pl.DeviceIdType.MESH)
    flips = []
    if scatter:
        bits = [lax.rem(m, 2), lax.rem(m // 2, 2), lax.rem(m // 4, 2)]
        flips = [m + (1 - 2 * bits[i]) * (1 << i) for i in range(3)]
        for f in flips:
            pl.semaphore_signal(barrier, inc=1, device_id={"grp": f},
                                device_id_type=pl.DeviceIdType.MESH)
    keys_t = jnp.concatenate([lat_t[0].astype(F32), jnp.zeros((pad, tok), F32)], axis=0)
    lat[0] = jnp.transpose(keys_t)[:, :kw].astype(BF)
    pl.semaphore_wait(barrier, n - 1 + len(flips))

    def key_copy(k):
        r = rows_of[k]
        return remote(lat.at[0, pl.ds(tok - r, r)], kbuf.at[k - 1, pl.ds(0, r)],
                      key_s.at[k - 1], key_r.at[k - 1], ctx=lax.rem(d + k, n))

    def id_copy(o):
        return remote(ids, idbuf.at[d], id_s.at[o - 1], id_r.at[o - 1], ctx=lax.rem(d + o, n))

    for k in range(1, reach):
        @pl.when(d + k < n)
        def _(k=k):
            key_copy(k).start()

    for o in range(1, n):
        id_copy(o).start()
    for k in range(1, reach):
        @pl.when(d - k < 0)
        def _(k=k):
            kbuf[k - 1] = jnp.zeros_like(kbuf[k - 1])
    idbuf[d] = ids[...]

    def repack(src, dst, width):
        group = 16 // qd

        def step(i, _):
            got = [
                src[0, :, pl.ds(pl.multiple_of((i * group + t) * width, 128), width)].astype(F32)
                for t in range(group)
            ]
            dst[pl.ds(pl.multiple_of(i * 16, 16), 16), :] = jnp.concatenate(got, axis=0).astype(BF)
            return 0

        lax.fori_loop(0, (HEADS // 2) // group, step, 0)

    copy_q.wait()
    repack(qraw, qs, pair)
    copy_g.wait()
    repack(graw, gs, 2 * LATENT)

    R = (HEADS // 2) * qd
    qrow = lax.broadcasted_iota(jnp.int32, (R, 1), 0) % qd
    own_ids = ids[...]
    qid = jnp.zeros((R, 1), jnp.int32)
    for i in range(qd):
        qid = jnp.where(qrow == i, own_ids[:, tok - qd + i:tok - qd + i + 1], qid)

    def query(par):
        return qs[:, 0:wide] if par == 0 else qs[:, pair - wide:pair]

    def grad(par):
        return gs[:, par * LATENT:(par + 1) * LATENT]

    def keys_of(k):
        return lat[0] if k == 0 else kbuf[k - 1, 0:rows_of[k], :]

    def block_products(k):
        kb = keys_of(k)
        zero = jnp.zeros((rows_of[k], pad), BF)
        padded = [jnp.concatenate([kb, zero], axis=1), jnp.concatenate([zero, kb], axis=1)]
        s = [dot(query(par), padded[par], ((1,), (1,))) for par in (0, 1)]
        dp = [dot(grad(par), kb[:, :LATENT], ((1,), (1,))) for par in (0, 1)]
        return s, dp

    products = [block_products(0)]

    for o in range(1, n):
        id_copy(o).wait_send()
        remote(ids, idbuf.at[lax.rem(d - o + n, n)], id_s.at[o - 1], id_r.at[o - 1],
               ctx=lax.rem(d + o, n)).wait_recv()
    for k in range(1, reach):
        @pl.when(d - k >= 0)
        def _(k=k):
            key_copy(k).wait_recv()
    for k in range(1, reach):
        products.append(block_products(k))

    allowed = []
    for k in range(reach):
        r = rows_of[k]
        row = own_ids if k == 0 else idbuf[jnp.maximum(d - k, 0)]
        row = row[:, tok - r:]
        lane = lax.broadcasted_iota(jnp.int32, (1, r), 1)
        ok = qid == row
        if k == 0:
            ok = ok & (lane <= tok - qd + qrow)
        else:
            reachable = jnp.where(lane + (tok - r) >= (k + 1) * tok - span, 1, 0)
            reachable = reachable * jnp.where(d - k >= 0, 1, 0)
            ok = ok & (reachable == 1)
        allowed.append(ok)

    dscores, probs = [[], []], [[], []]
    for par in (0, 1):
        s = [jnp.where(allowed[k], products[k][0][par] * score_scale, -1e30) for k in range(reach)]
        top = functools.reduce(jnp.maximum, [jnp.max(x, axis=1, keepdims=True) for x in s])
        w = [jnp.exp(x - top) for x in s]
        total = sum(jnp.sum(x, axis=1, keepdims=True) for x in w)
        w = [x / total for x in w]
        dps = [products[k][1][par] for k in range(reach)]
        rd = sum(jnp.sum(a * b, axis=1, keepdims=True) for a, b in zip(w, dps))
        for k in range(reach):
            dscores[par].append((w[k] * (dps[k] - rd) * score_scale).astype(BF))
            probs[par].append(w[k].astype(BF))

    def part_of(k):
        a = dot(dscores[0][k], query(0), ((0,), (0,)))[:, :kw]
        b = dot(dscores[1][k], query(1), ((0,), (0,)))[:, pad:pad + kw]
        v = dot(probs[0][k], grad(0), ((0,), (0,))) + dot(probs[1][k], grad(1), ((0,), (0,)))
        return (a + b + jnp.concatenate([v, jnp.zeros((rows_of[k], kw - LATENT), F32)], axis=1)).astype(BF)

    def part_copy(k, to):
        r = rows_of[k]
        return remote(psend.at[k - 1, pl.ds(0, r)], precv.at[k - 1, pl.ds(0, r)],
                      part_s.at[k - 1], part_r.at[k - 1], ctx=to)

    for k in range(1, reach):
        psend[k - 1, 0:rows_of[k], :] = part_of(k)

        @pl.when(d - k >= 0)
        def _(k=k):
            part_copy(k, jnp.maximum(d - k, 0)).start()

        @pl.when(d + k >= n)
        def _(k=k):
            precv[k - 1] = jnp.zeros_like(precv[k - 1])
    mine = part_of(0).astype(F32)

    eye = lax.broadcasted_iota(jnp.int32, (tok, tok), 0) == lax.broadcasted_iota(jnp.int32, (tok, tok), 1)
    doc_lane = lax.broadcasted_iota(jnp.int32, (1, 128), 1)
    member = []
    for j in range(n):
        col = jnp.sum(jnp.where(eye, idbuf[j], 0).astype(F32), axis=1, keepdims=True)
        member.append(jnp.where(col == doc_lane.astype(F32), 1.0, 0.0))

    for k in range(1, reach):
        @pl.when(d + k < n)
        def _(k=k):
            part_copy(k, jnp.maximum(d - k, 0)).wait_recv()
    for k in range(1, reach):
        r = rows_of[k]
        got = precv[k - 1, 0:r, :].astype(F32)
        if r < tok:
            got = jnp.concatenate([jnp.zeros((tok - r, kw), F32), got], axis=0)
        mine = mine + got
    mine_low = mine.astype(BF)
    full[d] = mine_low

    piece = tok // pieces

    def relay(direction, s, p):
        ss, rs = (up_s, up_r) if direction > 0 else (dn_s, dn_r)
        block = jnp.clip(d - direction * s, 0, n - 1)
        ref = full.at[block, pl.ds(p * piece, piece)]
        return remote(ref, ref, ss.at[s, p], rs.at[s, p], ctx=jnp.clip(d + direction, 0, n - 1))

    def arriving(direction, s, p):
        ss, rs = (up_s, up_r) if direction > 0 else (dn_s, dn_r)
        block = jnp.clip(d - direction * (s + 1), 0, n - 1)
        ref = full.at[block, pl.ds(p * piece, piece)]
        return remote(ref, ref, ss.at[s, p], rs.at[s, p], ctx=jnp.clip(d + direction, 0, n - 1))

    def can_send(direction, s):
        if direction > 0:
            return (d - s >= 0) & (d + 1 < n)
        return (d + s < n) & (d - 1 >= 0)

    def will_get(direction, s):
        return d - s - 1 >= 0 if direction > 0 else d + s + 1 < n

    for p in range(pieces):
        for direction in (1, -1):
            @pl.when(can_send(direction, 0))
            def _(p=p, direction=direction):
                relay(direction, 0, p).start()
    padded_out = jnp.concatenate([mine_low.astype(F32), jnp.zeros((tok, pad), F32)], axis=1)
    gk_out[0] = jnp.transpose(padded_out)[:kw].astype(BF)
    for s in range(n - 1):
        for p in range(pieces):
            for direction in (1, -1):
                @pl.when(will_get(direction, s))
                def _(p=p, s=s, direction=direction):
                    arriving(direction, s, p).wait_recv()
                if s + 1 < n - 1:
                    @pl.when(can_send(direction, s + 1))
                    def _(p=p, s=s, direction=direction):
                        relay(direction, s + 1, p).start()

    norms = jnp.zeros((1, 128), F32)
    for j in range(n):
        v = full[j].astype(F32)
        norms = norms + jnp.sum(member[j] * jnp.sum(v * v, axis=1, keepdims=True), axis=0, keepdims=True)
    limits = lim[...]
    if ndocs < 128:
        limits = jnp.concatenate([limits, jnp.zeros((1, 128 - ndocs), F32)], axis=1)
    factor = jnp.minimum(1.0, limits / jnp.sqrt(norms + norm_eps))
    share = kw // 8
    for j in range(n):
        f = jnp.sum(member[j] * factor, axis=1, keepdims=True)
        scaled = (full[j].astype(F32) * f).astype(BF).astype(F32)
        scaled = jnp.concatenate([scaled, jnp.zeros((tok, pad), F32)], axis=1)
        turned = jnp.transpose(scaled)
        if scatter:
            for b in range(8):
                scT[b % 2, (b // 2) * share:(b // 2 + 1) * share, j * tok:(j + 1) * tok] = (
                    turned[b * share:(b + 1) * share].astype(BF))
        else:
            scT[:, j * tok:(j + 1) * tok] = turned[:kw].astype(BF)

    copy_h.wait()
    if not scatter:
        w_out[...] = dot(scT[...], hid[0], ((1,), (0,)))
    else:
        chunks = col_chunks(w_out.shape[1])
        nc = len(chunks)
        bufs = [tail[7 * i:7 * i + 7] for i in range(nc)]
        rs_s, rs_r = tail[7 * nc:]
        core, xb, yb = bits

        def hop(i, stage):
            path = chunks[i][2]
            bit = 0 if stage == 0 else ((1, 2) if path == 0 else (2, 1))[stage - 1]
            s1, r1, acc, s2, r2, s3, r3 = bufs[i]
            src, dst = ((s1, r1), (s2, r2), (s3, r3))[stage]
            return remote(src, dst, rs_s.at[i, stage], rs_r.at[i, stage], grp=flips[bit])

        def block(path, moving, other):
            return other * 2 + moving if path == 0 else moving * 2 + other

        def product(i, half):
            start, width, _ = chunks[i]
            return dot(scT[half], hid[0, :, start:start + width], ((1,), (0,)))

        def send_first(i):
            bufs[i][0][...] = product(i, 1 - core).astype(BF)
            hop(i, 0).start()

        def own(i):
            bufs[i][2][...] = product(i, core).reshape(bufs[i][2].shape)

        def second(i):
            s1, r1, acc, s2, r2, s3, r3 = bufs[i]
            path = chunks[i][2]
            mb = xb if path == 0 else yb
            hop(i, 0).wait_recv()
            acc[...] = acc[...] + r1[...].astype(F32).reshape(acc.shape)
            for o in (0, 1):
                s2[o] = acc[block(path, 1 - mb, o)].astype(BF)
            hop(i, 1).start()

        def third(i):
            s1, r1, acc, s2, r2, s3, r3 = bufs[i]
            path = chunks[i][2]
            mb, ob = (xb, yb) if path == 0 else (yb, xb)
            hop(i, 1).wait_recv()
            s3[...] = (acc[block(path, mb, 1 - ob)] + r2[1 - ob].astype(F32)).astype(BF)
            hop(i, 2).start()

        def last(i):
            s1, r1, acc, s2, r2, s3, r3 = bufs[i]
            start, width, path = chunks[i]
            mb, ob = (xb, yb) if path == 0 else (yb, xb)
            kept = acc[block(path, mb, ob)] + r2[ob].astype(F32)
            hop(i, 2).wait_recv()
            w_out[:, start:start + width] = kept + r3[...].astype(F32)

        for i in range(0, nc, 2):
            for f in (send_first, own, second):
                f(i)
                f(i + 1)
        for f in (third, last):
            for i in range(nc):
                f(i)
        for i in range(nc):
            for stage in range(3):
                hop(i, stage).wait_send()

    for k in range(1, reach):
        @pl.when(d + k < n)
        def _(k=k):
            key_copy(k).wait_send()

        @pl.when(d - k >= 0)
        def _(k=k):
            part_copy(k, jnp.maximum(d - k, 0)).wait_send()
    for s in range(n - 1):
        for p in range(pieces):
            for direction in (1, -1):
                @pl.when(can_send(direction, s))
                def _(p=p, s=s, direction=direction):
                    relay(direction, s, p).wait_send()


def on_device(latent, queries, out_grad, hidden, doc_ids, clip_limits):
    n = lax.axis_size("ctx")
    groups = lax.axis_size("grp")
    tok, kw = latent.shape[1:]
    qd = queries.shape[1]
    seq = tok * n
    span = seq // 2 + qd
    reach = min(n, -(-span // tok))
    cols = hidden.shape[2]
    last = min(tok, -(-(span - (reach - 1) * tok) // 16) * 16)
    rows_of = [tok] * (reach - 1) + [last]
    ndocs = clip_limits.shape[1]
    scatter = groups == 8 and cols % 256 == 0 and cols >= 512 and kw % 64 == 0
    pieces = 2
    cfg = dict(n=n, tok=tok, kw=kw, qd=qd, reach=reach, rows_of=rows_of, span=span, ndocs=ndocs,
               pieces=pieces, scatter=scatter)
    rows = (HEADS // 2) * qd
    share = kw // 8
    dma = pltpu.SemaphoreType.DMA
    scratch = [
        pltpu.VMEM(queries.shape, BF),
        pltpu.VMEM(out_grad.shape, BF),
        pltpu.VMEM(hidden.shape, BF),
        pltpu.VMEM((rows, 2 * kw), BF),
        pltpu.VMEM((rows, 2 * LATENT), BF),
        pltpu.VMEM((reach - 1, tok, kw), BF),
        pltpu.VMEM((n, 1, tok), jnp.int32),
        pltpu.VMEM((reach - 1, tok, kw), BF),
        pltpu.VMEM((reach - 1, tok, kw), BF),
        pltpu.VMEM((n, tok, kw), BF),
        pltpu.VMEM((2, kw // 2, seq) if scatter else (kw, seq), BF),
        dma((3,)),
        dma((reach - 1,)), dma((reach - 1,)),
        dma((n - 1,)), dma((n - 1,)),
        dma((reach - 1,)), dma((reach - 1,)),
        dma((n - 1, pieces)), dma((n - 1, pieces)),
        dma((n - 1, pieces)), dma((n - 1, pieces)),
        pltpu.VMEM((1, tok, kw), BF),
    ]
    if scatter:
        chunks = col_chunks(cols)
        for _, w, _ in chunks:
            scratch += [
                pltpu.VMEM((kw // 2, w), BF), pltpu.VMEM((kw // 2, w), BF),
                pltpu.VMEM((4, share, w), F32),
                pltpu.VMEM((2, share, w), BF), pltpu.VMEM((2, share, w), BF),
                pltpu.VMEM((share, w), BF), pltpu.VMEM((share, w), BF),
            ]
        scratch += [dma((len(chunks), 3)), dma((len(chunks), 3))]
    vmem = pl.BlockSpec(memory_space=pltpu.VMEM)
    anywhere = pl.BlockSpec(memory_space=pl.ANY)
    grad_keys, weight = pl.pallas_call(
        functools.partial(body, cfg),
        out_shape=(
            jax.ShapeDtypeStruct((1, kw, tok), BF),
            jax.ShapeDtypeStruct((share if scatter else kw, cols), F32),
        ),
        in_specs=[vmem, vmem, vmem, anywhere, anywhere, anywhere],
        out_specs=(vmem, vmem),
        scratch_shapes=scratch,
        compiler_params=pltpu.CompilerParams(
            collective_id=0, has_side_effects=True, vmem_limit_bytes=60 * 1024 * 1024),
    )(jnp.swapaxes(latent, 1, 2), doc_ids, clip_limits, queries, out_grad, hidden)
    if not scatter:
        weight = lax.psum_scatter(weight, "grp", scatter_dimension=0, tiled=True)
    return (jnp.swapaxes(grad_keys, 1, 2), weight)


def solution(mesh):
    return jax.shard_map(
        on_device,
        mesh=mesh,
        in_specs=(
            P("grp", "ctx", None),
            P("grp", "ctx", None),
            P("grp", "ctx", None),
            P("grp", None, "ctx"),
            P("grp", "ctx"),
            P("grp", None),
        ),
        out_specs=(P("grp", "ctx", None), P("grp", "ctx")),
        check_vma=False,
    )
```

profile of v0, /device:TPU:0, one launch (start us, length us, event | category | flops | bytes accessed | tf_op | source)
XLA Modules:
  0.0 54.0 jit_solution(12091751876905542788)
XLA Ops:
  0.6 50.0 %shard_map.77 = (bf16[1,576,128]{2,1,0:T(8,128)(2,1)}, f32[72,1792]{1,0:T(8,128)}) custom-call(bf16[1,576,128]{2,1,0:T(8,128)(2,1)} %bitcast.2, s32[1,128]{1,0:T(1,128)} %refs_1_.1, f32[1,8]{1,0:T(1,128)} %refs_2_.1, bf16[1,4,73728]{2,1,0:T(4,128)(2,1)} %refs_3_.1, bf16[1,4,65536]{2,1,0:T(4,128)(2,1)} %refs_4_.1, bf16[1,512,1792]{2,1,0:T(8,128)(2,1)} %refs_5_.1), custom_call_target="tpu_custom_call" | custom-call | tf_op jit(solution)/shard_map/pallas_call | solution.py:429
  50.6 1.6 %copy.10 = bf16[1,128,576]{1,2,0:T(8,128)(2,1)} copy(bf16[1,128,576]{1,2,0:T(8,128)(2,1)} %bitcast.3) | data formatting | bytes 294912
  52.2 1.9 %copy.11 = f32[72,1792]{1,0:T(8,128)} copy(f32[72,1792]{1,0:T(8,128)} %get-tuple-element.9) | data formatting | bytes 1032192
where the time goes:
time: 54.2 us; the launch traced here: 54 us
  Pallas kernels  50 us (92%)
  local copies, waits for them, and re-layouts  3.44 us (6%)
  between operations  0.64 us (1%)
    pallas_call x1, Pallas kernels, on_device(): pl.pallas_call(functools.partial(body, cfg), out_shape=(jax.ShapeDtypeStr...  50 us
    unnamed x2, local copies, waits for them, and re-layouts  3.44 us

commit v1 on v0

--- a/solution.py
+++ b/solution.py
@@ -373,6 +373,15 @@
                 @pl.when(can_send(direction, s))
                 def _(p=p, s=s, direction=direction):
                     relay(direction, s, p).wait_send()
+
+
+def flush(gk, w, gk_out, w_out, sem):
+    a = pltpu.make_async_copy(gk, gk_out, sem.at[0])
+    b = pltpu.make_async_copy(w, w_out, sem.at[1])
+    a.start()
+    b.start()
+    a.wait()
+    b.wait()
 
 
 def on_device(latent, queries, out_grad, hidden, doc_ids, clip_limits):
@@ -429,6 +438,9 @@
     grad_keys, weight = pl.pallas_call(
         functools.partial(body, cfg),
         out_shape=(
+            pltpu.VMEM((1, kw, tok), BF),
+            pltpu.VMEM((share if scatter else kw, cols), F32),
+        ) if scatter else (
             jax.ShapeDtypeStruct((1, kw, tok), BF),
             jax.ShapeDtypeStruct((share if scatter else kw, cols), F32),
         ),

time: 54.2 us -> 51.4 us (0.948)
  local copies, waits for them, and re-layouts: 3.44 us -> 1.45 us
  Pallas kernels: 50 us -> 49.1 us
    unnamed x2, local copies, waits for them, and re-layouts: 3.44 us -> 1.45 us
    pallas_call x1, Pallas kernels: 50 us -> 49.1 us  [on_device(): pl.pallas_call(functools.partial(body, cfg), out_shape=(pltpu.VMEM((1, kw...]
where the time goes in v1:
time: 51.4 us; the launch traced here: 51.2 us
  Pallas kernels  49.1 us (96%)
  local copies, waits for them, and re-layouts  1.45 us (3%)
  between operations  0.64 us (1%)
    pallas_call x1, Pallas kernels, on_device(): pl.pallas_call(functools.partial(body, cfg), out_shape=(pltpu.VMEM((1, kw...  49.1 us
    unnamed x2, local copies, waits for them, and re-layouts  1.45 us

profile of v1, /device:TPU:0, one launch (start us, length us, event | category | flops | bytes accessed | tf_op | source)
XLA Modules:
  0.0 51.2 jit_solution(13323349109133757602)
XLA Ops:
  0.6 49.1 %shard_map.77 = (bf16[1,576,128]{2,1,0:T(8,128)(2,1)S(1)}, f32[72,1792]{1,0:T(8,128)S(1)}) custom-call(bf16[1,576,128]{2,1,0:T(8,128)(2,1)} %bitcast.3, s32[1,128]{1,0:T(1,128)} %refs_1_.1, f32[1,8]{1,0:T(1,128)} %refs_2_.1, bf16[1,4,73728]{2,1,0:T(4,128)(2,1)} %refs_3_.1, bf16[1,4,65536]{2,1,0:T(4,128)(2,1)} %refs_4_.1, bf16[1,512,1792]{2,1,0:T(8,128)(2,1)} %refs_5_.1), custom_call_target="tpu_custom_call" | custom-call | tf_op jit(solution)/shard_map/pallas_call | solution.py:438
  49.8 0.7 %copy.10 = bf16[1,128,576]{1,2,0:T(8,128)(2,1)} copy(bf16[1,128,576]{1,2,0:T(8,128)(2,1)S(1)} %bitcast.2) | data formatting | bytes 294912
  50.4 0.8 %copy.11 = f32[72,1792]{1,0:T(8,128)} copy(f32[72,1792]{1,0:T(8,128)S(1)} %get-tuple-element.7) | data formatting | bytes 1032192

commit v2 on v1

--- a/solution.py
+++ b/solution.py
@@ -21,16 +21,6 @@
 
 def dot(a, b, dims):
     return lax.dot_general(a, b, (dims, ((), ())), preferred_element_type=F32)
-
-
-def col_chunks(cols):
-    half = cols // 2
-    first = -(-(half // 2) // 128) * 128
-    out = []
-    for start, width in ((0, first), (first, half - first)):
-        for path in (0, 1):
-            out.append((path * half + start, width, path))
-    return out
 
 
 def body(cfg, *refs):
@@ -43,13 +33,10 @@
     span = cfg["span"]
     ndocs = cfg["ndocs"]
     pieces = cfg["pieces"]
-    scatter = cfg["scatter"]
     (lat_t, ids, lim, q_hbm, g_hbm, h_hbm, gk_out, w_out) = refs[:8]
     (qraw, graw, hid, qs, gs, kbuf, idbuf, psend, precv, full, scT, local_sem, key_s, key_r,
      id_s, id_r, part_s, part_r, up_s, up_r, dn_s, dn_r, lat) = refs[8:31]
-    tail = refs[31:]
     d = lax.axis_index("ctx")
-    m = lax.axis_index("grp")
     wide = -(-kw // 128) * 128
     pad = wide - kw
     pair = 2 * kw
@@ -72,16 +59,9 @@
     for o in range(1, n):
         pl.semaphore_signal(barrier, inc=1, device_id={"ctx": lax.rem(d + o, n)},
                             device_id_type=pl.DeviceIdType.MESH)
-    flips = []
-    if scatter:
-        bits = [lax.rem(m, 2), lax.rem(m // 2, 2), lax.rem(m // 4, 2)]
-        flips = [m + (1 - 2 * bits[i]) * (1 << i) for i in range(3)]
-        for f in flips:
-            pl.semaphore_signal(barrier, inc=1, device_id={"grp": f},
-                                device_id_type=pl.DeviceIdType.MESH)
     keys_t = jnp.concatenate([lat_t[0].astype(F32), jnp.zeros((pad, tok), F32)], axis=0)
     lat[0] = jnp.transpose(keys_t)[:, :kw].astype(BF)
-    pl.semaphore_wait(barrier, n - 1 + len(flips))
+    pl.semaphore_wait(barrier, n - 1)
 
     def key_copy(k):
         r = rows_of[k]
@@ -278,86 +258,15 @@
     if ndocs < 128:
         limits = jnp.concatenate([limits, jnp.zeros((1, 128 - ndocs), F32)], axis=1)
     factor = jnp.minimum(1.0, limits / jnp.sqrt(norms + norm_eps))
-    share = kw // 8
     for j in range(n):
         f = jnp.sum(member[j] * factor, axis=1, keepdims=True)
         scaled = (full[j].astype(F32) * f).astype(BF).astype(F32)
         scaled = jnp.concatenate([scaled, jnp.zeros((tok, pad), F32)], axis=1)
         turned = jnp.transpose(scaled)
-        if scatter:
-            for b in range(8):
-                scT[b % 2, (b // 2) * share:(b // 2 + 1) * share, j * tok:(j + 1) * tok] = (
-                    turned[b * share:(b + 1) * share].astype(BF))
-        else:
-            scT[:, j * tok:(j + 1) * tok] = turned[:kw].astype(BF)
+        scT[:, j * tok:(j + 1) * tok] = turned[:kw].astype(BF)
 
     copy_h.wait()
-    if not scatter:
-        w_out[...] = dot(scT[...], hid[0], ((1,), (0,)))
-    else:
-        chunks = col_chunks(w_out.shape[1])
-        nc = len(chunks)
-        bufs = [tail[7 * i:7 * i + 7] for i in range(nc)]
-        rs_s, rs_r = tail[7 * nc:]
-        core, xb, yb = bits
-
-        def hop(i, stage):
-            path = chunks[i][2]
-            bit = 0 if stage == 0 else ((1, 2) if path == 0 else (2, 1))[stage - 1]
-            s1, r1, acc, s2, r2, s3, r3 = bufs[i]
-            src, dst = ((s1, r1), (s2, r2), (s3, r3))[stage]
-            return remote(src, dst, rs_s.at[i, stage], rs_r.at[i, stage], grp=flips[bit])
-
-        def block(path, moving, other):
-            return other * 2 + moving if path == 0 else moving * 2 + other
-
-        def product(i, half):
-            start, width, _ = chunks[i]
-            return dot(scT[half], hid[0, :, start:start + width], ((1,), (0,)))
-
-        def send_first(i):
-            bufs[i][0][...] = product(i, 1 - core).astype(BF)
-            hop(i, 0).start()
-
-        def own(i):
-            bufs[i][2][...] = product(i, core).reshape(bufs[i][2].shape)
-
-        def second(i):
-            s1, r1, acc, s2, r2, s3, r3 = bufs[i]
-            path = chunks[i][2]
-            mb = xb if path == 0 else yb
-            hop(i, 0).wait_recv()
-            acc[...] = acc[...] + r1[...].astype(F32).reshape(acc.shape)
-            for o in (0, 1):
-                s2[o] = acc[block(path, 1 - mb, o)].astype(BF)
-            hop(i, 1).start()
-
-        def third(i):
-            s1, r1, acc, s2, r2, s3, r3 = bufs[i]
-            path = chunks[i][2]
-            mb, ob = (xb, yb) if path == 0 else (yb, xb)
-            hop(i, 1).wait_recv()
-            s3[...] = (acc[block(path, mb, 1 - ob)] + r2[1 - ob].astype(F32)).astype(BF)
-            hop(i, 2).start()
-
-        def last(i):
-            s1, r1, acc, s2, r2, s3, r3 = bufs[i]
-            start, width, path = chunks[i]
-            mb, ob = (xb, yb) if path == 0 else (yb, xb)
-            kept = acc[block(path, mb, ob)] + r2[ob].astype(F32)
-            hop(i, 2).wait_recv()
-            w_out[:, start:start + width] = kept + r3[...].astype(F32)
-
-        for i in range(0, nc, 2):
-            for f in (send_first, own, second):
-                f(i)
-                f(i + 1)
-        for f in (third, last):
-            for i in range(nc):
-                f(i)
-        for i in range(nc):
-            for stage in range(3):
-                hop(i, stage).wait_send()
+    w_out[...] = dot(scT[...], hid[0], ((1,), (0,)))
 
     for k in range(1, reach):
         @pl.when(d + k < n)
@@ -382,6 +291,557 @@
     b.start()
     a.wait()
     b.wait()
+
+
+def pair_body(cfg, *refs):
+    n = cfg["n"]
+    tok = cfg["tok"]
+    kw = cfg["kw"]
+    qd = cfg["qd"]
+    halo = cfg["halo"]
+    ndocs = cfg["ndocs"]
+    splits = cfg["splits"]
+    seq = n * tok
+    wide = -(-kw // 128) * 128
+    pad = wide - kw
+    share = kw // 8
+    np_ = len(splits)
+    offs = [sum(splits[:p]) for p in range(np_)]
+    (lat_hbm, ids_hbm, lim_hbm, q_hbm, g_hbm, h_hbm, gk_out, w_out,
+     lat_t, lat, ids, lim, qraw, graw, hid, qs, gs, kbuf, krot, kgot, lath, hkey, idbuf,
+     psend, precv, hsend, hrecv, ownb, own2, full, gkr, nbuf, lhs,
+     loc, id_s, id_r, key_s, key_r, hid_s, hid_r, part_s, part_r, halo_s, halo_r,
+     own_s, own_r, gk_s, gk_r, nrm_s, nrm_r, blk_s, blk_r, rs_s, rs_r) = refs[:54]
+    tail = refs[54:]
+    d = lax.axis_index("ctx")
+    m = lax.axis_index("grp")
+    c = lax.rem(m, 2)
+    xb = lax.rem(m // 2, 2)
+    yb = lax.rem(m // 4, 2)
+    base = m - c
+    mate = base + 1 - c
+    flip_x = m + 2 - 4 * xb
+    flip_y = m + 4 - 8 * yb
+    cols = w_out.shape[1]
+    wing = cols // 2
+
+    def remote(src, dst, ss, rs, **where):
+        return pltpu.make_async_remote_copy(
+            src_ref=src, dst_ref=dst, send_sem=ss, recv_sem=rs,
+            device_id=where, device_id_type=pl.DeviceIdType.MESH,
+        )
+
+    loads = [
+        pltpu.make_async_copy(lat_hbm, lat_t, loc.at[0]),
+        pltpu.make_async_copy(ids_hbm, ids, loc.at[1]),
+        pltpu.make_async_copy(q_hbm, qraw, loc.at[2]),
+        pltpu.make_async_copy(g_hbm, graw, loc.at[3]),
+        pltpu.make_async_copy(lim_hbm, lim, loc.at[4]),
+        pltpu.make_async_copy(h_hbm.at[0], hid.at[c], loc.at[5]),
+    ]
+    for copy in loads:
+        copy.start()
+
+    barrier = pltpu.get_barrier_semaphore()
+
+    def greet(**where):
+        pl.semaphore_signal(barrier, inc=1, device_id=where, device_id_type=pl.DeviceIdType.MESH)
+
+    for o in range(n):
+        if o:
+            greet(ctx=lax.rem(d + o, n), grp=m)
+        greet(ctx=lax.rem(d + o, n), grp=mate)
+    greet(grp=flip_x)
+    greet(grp=flip_y)
+
+    loads[0].wait()
+    keys_t = jnp.concatenate([lat_t[0].astype(F32), jnp.zeros((pad, tok), F32)], axis=0)
+    keys = jnp.transpose(keys_t)
+    lat[...] = keys.astype(BF)
+    near = tok // 2
+    rope = kw - LATENT
+    krot[...] = jnp.concatenate([keys[:near, LATENT:kw], keys[near:, LATENT:kw]], axis=1).astype(BF)
+    lath[...] = keys[tok - halo:].astype(BF)
+    loads[1].wait()
+    pl.semaphore_wait(barrier, 2 * n + 1)
+
+    def id_copy(k):
+        return remote(ids, idbuf.at[k - 1], id_s.at[k - 1], id_r.at[k - 1], ctx=lax.rem(d + k, n))
+
+    def key_copy(k):
+        if k == 1:
+            return [
+                remote(lat.at[:, pl.ds(0, LATENT)], kbuf.at[pl.ds(0, tok), pl.ds(0, LATENT)],
+                       key_s.at[0], key_r.at[0], ctx=lax.rem(d + 1, n)),
+                remote(krot, kgot, key_s.at[2], key_r.at[2], ctx=lax.rem(d + 1, n)),
+            ]
+        return [remote(lath, hkey, key_s.at[1], key_r.at[1], ctx=lax.rem(d + 2, n))]
+
+    for k in (2, 1):
+        @pl.when(d + k < n)
+        def _(k=k):
+            id_copy(k).start()
+            for copy in key_copy(k):
+                copy.start()
+
+    hid_copy = remote(h_hbm.at[0], hid.at[c], hid_s.at[0], hid_r.at[0], grp=mate)
+    hid_copy.start()
+
+    @pl.when(d < 1)
+    def _():
+        kbuf[0:tok, :] = jnp.zeros((tok, wide), BF)
+        kgot[...] = jnp.zeros_like(kgot)
+        idbuf[0] = jnp.zeros_like(idbuf[0])
+
+    @pl.when(d < 2)
+    def _():
+        hkey[...] = jnp.zeros_like(hkey)
+        idbuf[1] = jnp.zeros_like(idbuf[1])
+
+    group = 16 // qd
+    R = (HEADS // 2) * qd
+
+    def repack(src, dst, width):
+        def step(i, _):
+            got = [
+                src[0, :, pl.ds(pl.multiple_of((i * group + t) * 2 * width, 128), 2 * width)].astype(F32)
+                for t in range(group)
+            ]
+            got = jnp.concatenate(got, axis=0)
+            for par in (0, 1):
+                one = got[:, par * width:(par + 1) * width]
+                if width % 128:
+                    one = jnp.concatenate([one, jnp.zeros((16, pad), F32)], axis=1)
+                dst[pl.ds(pl.multiple_of(par * R + i * 16, 16), 16), :] = one.astype(BF)
+            return 0
+
+        lax.fori_loop(0, (HEADS // 2) // group, step, 0)
+
+    loads[2].wait()
+    repack(qraw, qs, kw)
+    loads[3].wait()
+    repack(graw, gs, LATENT)
+
+    def turn_ids(row):
+        return jnp.transpose(jnp.broadcast_to(row.astype(F32), (tok, tok)))
+
+    def across(x):
+        return jnp.concatenate([x] * (2 * R // tok), axis=1)
+
+    qrow = lax.broadcasted_iota(jnp.int32, (1, tok), 1) % qd
+    own_ids = ids[...]
+    qid = jnp.zeros((1, tok), F32)
+    for i in range(qd):
+        qid = jnp.where(qrow == i, own_ids[:, tok - qd + i:tok - qd + i + 1].astype(F32), qid)
+
+    def block_products(keys):
+        return (dot(keys, qs[...], ((1,), (1,))), dot(keys[:, :LATENT], gs[...], ((1,), (1,))))
+
+    key_row = lax.broadcasted_iota(jnp.int32, (tok, tok), 0)
+    s0, dp0 = block_products(lat[...])
+    ok0 = jnp.where(turn_ids(own_ids) == qid, 1, 0) * jnp.where(key_row <= tok - qd + qrow, 1, 0)
+    s0 = jnp.where(across(ok0) == 1, s0 * score_scale, -1e30)
+    top0 = jnp.max(s0, axis=0, keepdims=True)
+
+    for k in (2, 1):
+        @pl.when(d >= k)
+        def _(k=k):
+            id_copy(k).wait_recv()
+            for copy in key_copy(k):
+                copy.wait_recv()
+    got = kgot[...].astype(F32)
+    got = jnp.concatenate([got[:, :rope], got[:, rope:]], axis=0)
+    kbuf[0:tok, LATENT:wide] = jnp.concatenate([got, jnp.zeros((tok, wide - kw), F32)], axis=1).astype(BF)
+    kbuf[tok:tok + 16, :] = jnp.concatenate([jnp.zeros((16 - halo, wide), F32), hkey[...].astype(F32)], axis=0).astype(BF)
+    s1, dp1 = block_products(kbuf[...])
+    ok1 = jnp.where(turn_ids(idbuf[0]) == qid, 1, 0)
+    ok1 = ok1 * jnp.where(key_row >= 2 * tok - cfg["span"], 1, 0) * jnp.where(d >= 1, 1, 0)
+    ok2 = jnp.where(turn_ids(idbuf[1]) == qid, 1, 0)
+    ok2 = ok2 * jnp.where(key_row >= 3 * tok - cfg["span"], 1, 0) * jnp.where(d >= 2, 1, 0)
+    ok1 = jnp.concatenate([ok1, ok2[tok - 16:]], axis=0)
+    s1 = jnp.where(across(ok1) == 1, s1 * score_scale, -1e30)
+    top = jnp.maximum(top0, jnp.max(s1, axis=0, keepdims=True))
+    w0, w1 = jnp.exp(s0 - top), jnp.exp(s1 - top)
+    scale = 1.0 / (jnp.sum(w0, axis=0, keepdims=True) + jnp.sum(w1, axis=0, keepdims=True))
+    w0, w1 = w0 * scale, w1 * scale
+    rd = jnp.sum(w0 * dp0, axis=0, keepdims=True) + jnp.sum(w1 * dp1, axis=0, keepdims=True)
+
+    def part_of(w, dp):
+        a = dot((w * (dp - rd) * score_scale).astype(BF), qs[...], ((1,), (0,)))
+        v = dot(w.astype(BF), gs[...], ((1,), (0,)))
+        return a + jnp.concatenate([v, jnp.zeros((v.shape[0], wide - LATENT), F32)], axis=1)
+
+    def halves(turned):
+        out = []
+        for h in (0, 1):
+            rows = []
+            for p in range(np_):
+                for q in range(4):
+                    start = share * (2 * q + h) + offs[p]
+                    rows.append(turned[start:start + splits[p]])
+            out.append(jnp.concatenate(rows, axis=0))
+        return out
+
+    def halo_copy(h):
+        return remote(hsend, hrecv.at[c], halo_s.at[h], halo_r.at[c],
+                      ctx=jnp.maximum(d - 2, 0), grp=base + h)
+
+    def part_copy(h, p):
+        rows = pl.ds(4 * offs[p], 4 * splits[p])
+        return remote(psend.at[h, rows], precv.at[c, rows], part_s.at[h, p], part_r.at[c, p],
+                      ctx=jnp.maximum(d - 1, 0), grp=base + h)
+
+    part1 = part_of(w1, dp1)
+    hsend[...] = part1[tok + 16 - halo:].astype(BF)
+
+    @pl.when(d >= 2)
+    def _():
+        for h in (0, 1):
+            halo_copy(h).start()
+
+    turned = halves(jnp.transpose(part1[:tok]))
+    for h in (0, 1):
+        psend[h] = turned[h].astype(BF)
+
+    @pl.when(d >= 1)
+    def _():
+        for p in range(np_):
+            for h in (0, 1):
+                part_copy(h, p).start()
+
+    @pl.when(d + 1 >= n)
+    def _():
+        precv[...] = jnp.zeros_like(precv)
+
+    @pl.when(d + 2 >= n)
+    def _():
+        hrecv[...] = jnp.zeros_like(hrecv)
+
+    turned = halves(jnp.transpose(part_of(w0, dp0)))
+    for h in (0, 1):
+        ownb[h] = turned[h].astype(BF)
+    own_copy = remote(ownb.at[1 - c], own2.at[c], own_s.at[0], own_r.at[0], grp=mate)
+    own_copy.start()
+    own2[c] = ownb[c]
+    own_copy.wait_recv()
+
+    def rows_at(p):
+        return pl.ds(8 * offs[p], 8 * splits[p])
+
+    steps = (-1, 1, -2, 2)
+
+    def spread(o, p):
+        i = steps.index(o)
+        ref = full.at[d, rows_at(p)]
+        return remote(ref, ref, blk_s.at[i, p], blk_r.at[i, p], ctx=jnp.clip(d + o, 0, n - 1))
+
+    def spread_from(o, p):
+        i = steps.index(o)
+        ref = full.at[jnp.clip(d - o, 0, n - 1), rows_at(p)]
+        return remote(ref, ref, blk_s.at[i, p], blk_r.at[i, p], ctx=jnp.clip(d - o, 0, n - 1))
+
+    def pass_end(o, p):
+        i = 4 if o < 0 else 5
+        ref = full.at[n - 1 if o < 0 else 0, rows_at(p)]
+        return remote(ref, ref, blk_s.at[i, p], blk_r.at[i, p], ctx=jnp.clip(d + o, 0, n - 1))
+
+    def reaches(o):
+        return (d + o >= 0) & (d + o < n)
+
+    def comes(o):
+        return (d - o >= 0) & (d - o < n)
+
+    def passes(o):
+        return d == (1 if o < 0 else n - 2)
+
+    def ends(o):
+        return d == (0 if o < 0 else n - 1)
+
+    def halo_from(g):
+        return remote(hsend, hrecv.at[g], halo_s.at[0], halo_r.at[g], grp=mate)
+
+    def part_from(g, p):
+        rows = pl.ds(4 * offs[p], 4 * splits[p])
+        return remote(psend.at[0, rows], precv.at[g, rows], part_s.at[0, p], part_r.at[g, p], grp=mate)
+
+    @pl.when(d + 2 < n)
+    def _():
+        for g in (0, 1):
+            halo_from(g).wait_recv()
+
+    side = []
+    for g in (0, 1):
+        block = jnp.concatenate([jnp.zeros((tok - halo, wide), F32), hrecv[g].astype(F32)], axis=0)
+        turned = halves(jnp.transpose(block))
+        side.append(jnp.where(c == 0, turned[0], turned[1]))
+
+    def spread_all(p):
+        for o in steps:
+            @pl.when(reaches(o))
+            def _(o=o):
+                spread(o, p).start()
+
+    token_norm = [jnp.zeros((1, tok), F32) for _ in (0, 1)]
+    for p in range(np_):
+        @pl.when(d + 1 < n)
+        def _(p=p):
+            for g in (0, 1):
+                part_from(g, p).wait_recv()
+        lo, size = 4 * offs[p], 4 * splits[p]
+        for g in (0, 1):
+            value = own2[g, lo:lo + size].astype(F32) + precv[g, lo:lo + size].astype(F32)
+            value = (value + side[g][lo:lo + size]).astype(BF)
+            full[d, 2 * lo + g * size:2 * lo + (g + 1) * size] = value
+            value = value.astype(F32)
+            token_norm[g] = token_norm[g] + jnp.sum(value * value, axis=0, keepdims=True)
+        if p == 0:
+            spread_all(p)
+
+    loads[4].wait()
+    limits = jnp.concatenate([lim[...], jnp.zeros((1, tok - ndocs), F32)], axis=1)
+    nbuf[c, d] = jnp.concatenate(
+        token_norm + [own_ids.astype(F32), limits, jnp.zeros((4, tok), F32)], axis=0)
+
+    def norm_copy(o, flip):
+        i = 2 * o + flip - 1
+        ref = nbuf.at[c, d]
+        return remote(ref, ref, nrm_s.at[i], nrm_r.at[i], ctx=lax.rem(d + o, n), grp=mate if flip else m)
+
+    def norm_from(o, flip):
+        i = 2 * o + flip - 1
+        ref = nbuf.at[1 - c if flip else c, lax.rem(d - o + n, n)]
+        return remote(ref, ref, nrm_s.at[i], nrm_r.at[i], ctx=lax.rem(d + o, n), grp=mate if flip else m)
+
+    peers = [(o, flip) for o in range(n) for flip in (0, 1) if o or flip]
+    for o, flip in peers:
+        norm_copy(o, flip).start()
+    for p in range(1, np_):
+        spread_all(p)
+
+    def gk_copy(p):
+        lo, size = 4 * offs[p], 4 * splits[p]
+        src = full.at[d, pl.ds(pl.multiple_of(2 * lo + (1 - c) * size, 16), size)]
+        return remote(src, gkr.at[pl.ds(lo, size)], gk_s.at[p], gk_r.at[p], grp=mate)
+
+    for p in range(np_):
+        gk_copy(p).start()
+
+    factors = []
+
+    def make_factors():
+        for o, flip in peers:
+            norm_from(o, flip).wait_recv()
+        rows = -(-ndocs // 8) * 8
+        sub = lax.broadcasted_iota(jnp.int32, (rows, tok), 0).astype(F32)
+        lane = lax.broadcasted_iota(jnp.int32, (rows, tok), 1).astype(F32)
+        for g in (0, 1):
+            member = [jnp.where(nbuf[g, b, 2:3] == sub, 1.0, 0.0) for b in range(n)]
+            norms = sum(
+                jnp.sum(member[b] * (nbuf[0, b, g:g + 1] + nbuf[1, b, g:g + 1]), axis=1, keepdims=True)
+                for b in range(n))
+            top = jnp.sum(jnp.where(lane == sub, nbuf[g, 0, 3:4], 0.0), axis=1, keepdims=True)
+            factor = jnp.minimum(1.0, top / jnp.sqrt(norms + norm_eps))
+            factors.append([jnp.sum(member[b] * factor, axis=0, keepdims=True) for b in range(n)])
+
+    def forward(p):
+        for o in (-1, 1):
+            @pl.when(passes(o))
+            def _(o=o):
+                spread_from(2 * o, p).wait_recv()
+                pass_end(o, p).start()
+
+    def gather(p):
+        for o in steps:
+            keep = comes(o)
+            if o in (-2, 2):
+                keep = keep & jnp.logical_not(passes(o // 2))
+
+            @pl.when(keep)
+            def _(o=o):
+                spread_from(o, p).wait_recv()
+        for o in (-1, 1):
+            @pl.when(ends(o))
+            def _(o=o):
+                pass_end(o, p).wait_recv()
+
+    bufs = [[tail[5 * (2 * p + w):5 * (2 * p + w) + 5] for w in (0, 1)] for p in range(np_)]
+
+    def hop(p, w, stage):
+        first, back, second, back2, _ = bufs[p][w]
+        where = (flip_x, flip_y) if w == 0 else (flip_y, flip_x)
+        src, dst = (first, back) if stage == 0 else (second, back2)
+        return remote(src, dst, rs_s.at[p, w, stage], rs_r.at[p, w, stage], grp=where[stage])
+
+    def chip(w, moving, other):
+        return other * 2 + moving if w == 0 else moving * 2 + other
+
+    def product(p):
+        lo, size = 4 * offs[p], 4 * splits[p]
+        for g in (0, 1):
+            for b in range(n):
+                value = full[b, 2 * lo + g * size:2 * lo + (g + 1) * size].astype(F32)
+                at = (g * n + b) * tok
+                lhs[lo:lo + size, at:at + tok] = (value * factors[g][b]).astype(BF)
+        for w in (0, 1):
+            first, _, _, _, total = bufs[p][w]
+            out = sum(
+                dot(lhs[lo:lo + size, g * seq:(g + 1) * seq], hid[g, :, w * wing:(w + 1) * wing], ((1,), (0,)))
+                for g in (0, 1))
+            total[...] = out.reshape(total.shape)
+            mb = xb if w == 0 else yb
+            for o in (0, 1):
+                first[o] = total[chip(w, 1 - mb, o)].astype(BF)
+            hop(p, w, 0).start()
+
+    def pass_on(p):
+        for w in (0, 1):
+            _, back, second, _, total = bufs[p][w]
+            mb, ob = (xb, yb) if w == 0 else (yb, xb)
+            hop(p, w, 0).wait_recv()
+            second[...] = (total[chip(w, mb, 1 - ob)] + back[1 - ob].astype(F32)).astype(BF)
+            hop(p, w, 1).start()
+
+    def last(p):
+        for w in (0, 1):
+            _, back, _, back2, total = bufs[p][w]
+            mb, ob = (xb, yb) if w == 0 else (yb, xb)
+            kept = total[chip(w, mb, ob)] + back[ob].astype(F32)
+            hop(p, w, 1).wait_recv()
+            w_out[offs[p]:offs[p] + splits[p], w * wing:(w + 1) * wing] = kept + back2[...].astype(F32)
+
+    def write_keys():
+        for p in range(np_):
+            gk_copy(p).wait_recv()
+        order = [None] * (8 * np_)
+        for p in range(np_):
+            lo, size = 4 * offs[p], splits[p]
+            near = [full[d, 2 * lo + g * 4 * size:2 * lo + (g + 1) * 4 * size].astype(F32) for g in (0, 1)]
+            near = jnp.where(c == 0, near[0], near[1])
+            far = gkr[lo:lo + 4 * size].astype(F32)
+            for h in (0, 1):
+                value = jnp.where(c == h, near, far)
+                for q in range(4):
+                    order[(2 * q + h) * np_ + p] = value[q * size:(q + 1) * size]
+        gk_out[0] = jnp.concatenate(order, axis=0).astype(BF)
+
+    forward(0)
+    make_factors()
+    loads[5].wait()
+    hid_copy.wait_recv()
+    for p in range(np_):
+        if p + 1 < np_:
+            forward(p + 1)
+        gather(p)
+        product(p)
+        if p == 0:
+            write_keys()
+        if p >= 1:
+            pass_on(p - 1)
+        if p >= 2:
+            last(p - 2)
+    pass_on(np_ - 1)
+    if np_ >= 2:
+        last(np_ - 2)
+    last(np_ - 1)
+
+    for k in (1, 2):
+        @pl.when(d + k < n)
+        def _(k=k):
+            id_copy(k).wait_send()
+            for copy in key_copy(k):
+                copy.wait_send()
+    hid_copy.wait_send()
+
+    @pl.when(d >= 2)
+    def _():
+        for h in (0, 1):
+            halo_copy(h).wait_send()
+
+    @pl.when(d >= 1)
+    def _():
+        for p in range(np_):
+            for h in (0, 1):
+                part_copy(h, p).wait_send()
+    own_copy.wait_send()
+    for p in range(np_):
+        gk_copy(p).wait_send()
+    for o, flip in peers:
+        norm_copy(o, flip).wait_send()
+    for p in range(np_):
+        for o in steps:
+            @pl.when(reaches(o))
+            def _(p=p, o=o):
+                spread(o, p).wait_send()
+        for o in (-1, 1):
+            @pl.when(passes(o))
+            def _(p=p, o=o):
+                pass_end(o, p).wait_send()
+    for p in range(np_):
+        for w in (0, 1):
+            for stage in (0, 1):
+                hop(p, w, stage).wait_send()
+
+
+def pair_scratch(cfg, latent, queries, out_grad, hidden, clip_limits):
+    n, tok, kw, halo = cfg["n"], cfg["tok"], cfg["kw"], cfg["halo"]
+    splits = cfg["splits"]
+    np_ = len(splits)
+    half = kw // 2
+    wide = -(-kw // 128) * 128
+    rows = (HEADS // 2) * cfg["qd"]
+    cols = hidden.shape[2]
+    seq = n * tok
+    dma = pltpu.SemaphoreType.DMA
+    v = pltpu.VMEM
+    scratch = [
+        v((1, kw, tok), BF), v((tok, wide), BF), v((1, tok), jnp.int32), v(clip_limits.shape, F32),
+        v(queries.shape, BF), v(out_grad.shape, BF), v((2, seq, cols), BF),
+        v((2 * rows, wide), BF), v((2 * rows, LATENT), BF),
+        v((tok + 16, wide), BF), v((tok // 2, 2 * (kw - LATENT)), BF), v((tok // 2, 2 * (kw - LATENT)), BF),
+        v((halo, wide), BF), v((halo, wide), BF), v((2, 1, tok), jnp.int32),
+        v((2, half, tok), BF), v((2, half, tok), BF), v((halo, wide), BF), v((2, halo, wide), BF),
+        v((2, half, tok), BF), v((2, half, tok), BF), v((n, kw, tok), BF), v((half, tok), BF),
+        v((2, n, 8, tok), F32), v((half, 2 * seq), BF),
+        dma((6,)), dma((2,)), dma((2,)), dma((3,)), dma((3,)), dma((1,)), dma((1,)),
+        dma((2, np_)), dma((2, np_)), dma((2,)), dma((2,)),
+        dma((1,)), dma((1,)), dma((np_,)), dma((np_,)),
+        dma((2 * n,)), dma((2 * n,)),
+        dma((6, np_)), dma((6, np_)),
+        dma((np_, 2, 2)), dma((np_, 2, 2)),
+    ]
+    for size in splits:
+        for _ in (0, 1):
+            scratch += [
+                v((2, size, cols // 2), BF), v((2, size, cols // 2), BF),
+                v((size, cols // 2), BF), v((size, cols // 2), BF),
+                v((4, size, cols // 2), F32),
+            ]
+    return scratch
+
+
+def row_splits(share):
+    units = share // 8
+    cuts = [0] + [units * p // 9 for p in (3, 6)] + [units]
+    return tuple(8 * (b - a) for a, b in zip(cuts, cuts[1:]) if b > a)
+
+
+def pair_call(cfg, latent, queries, out_grad, hidden, doc_ids, clip_limits):
+    anywhere = pl.BlockSpec(memory_space=pl.ANY)
+    vmem = pl.BlockSpec(memory_space=pltpu.VMEM)
+    tok, kw = cfg["tok"], cfg["kw"]
+    grad_keys, weight = pl.pallas_call(
+        functools.partial(pair_body, cfg),
+        out_shape=(
+            pltpu.VMEM((1, kw, tok), BF),
+            pltpu.VMEM((kw // 8, hidden.shape[2]), F32),
+        ),
+        in_specs=[anywhere] * 6,
+        out_specs=(vmem, vmem),
+        scratch_shapes=pair_scratch(cfg, latent, queries, out_grad, hidden, clip_limits),
+        compiler_params=pltpu.CompilerParams(
+            collective_id=0, has_side_effects=True, vmem_limit_bytes=56 * 1024 * 1024),
+    )(jnp.swapaxes(latent, 1, 2), doc_ids, clip_limits, queries, out_grad, hidden)
+    return (jnp.swapaxes(grad_keys, 1, 2), weight)
 
 
 def on_device(latent, queries, out_grad, hidden, doc_ids, clip_limits):
@@ -396,12 +856,16 @@
     last = min(tok, -(-(span - (reach - 1) * tok) // 16) * 16)
     rows_of = [tok] * (reach - 1) + [last]
     ndocs = clip_limits.shape[1]
-    scatter = groups == 8 and cols % 256 == 0 and cols >= 512 and kw % 64 == 0
+    share = kw // 8
+    paired = (groups == 8 and n == 4 and reach == 3 and last <= tok and cols % 256 == 0 and kw % 64 == 0
+              and tok % 128 == 0 and ndocs <= tok and span <= 2 * tok + 16 and 2 * (kw - LATENT) == 128)
+    if paired:
+        cfg = dict(n=n, tok=tok, kw=kw, qd=qd, halo=-(-(span - 2 * tok) // 4) * 4, span=span, ndocs=ndocs, splits=row_splits(share))
+        return pair_call(cfg, latent, queries, out_grad, hidden, doc_ids, clip_limits)
     pieces = 2
     cfg = dict(n=n, tok=tok, kw=kw, qd=qd, reach=reach, rows_of=rows_of, span=span, ndocs=ndocs,
-               pieces=pieces, scatter=scatter)
+               pieces=pieces)
     rows = (HEADS // 2) * qd
-    share = kw // 8
     dma = pltpu.SemaphoreType.DMA
     scratch = [
         pltpu.VMEM(queries.shape, BF),
@@ -414,7 +878,7 @@
         pltpu.VMEM((reach - 1, tok, kw), BF),
         pltpu.VMEM((reach - 1, tok, kw), BF),
         pltpu.VMEM((n, tok, kw), BF),
-        pltpu.VMEM((2, kw // 2, seq) if scatter else (kw, seq), BF),
+        pltpu.VMEM((kw, seq), BF),
         dma((3,)),
         dma((reach - 1,)), dma((reach - 1,)),
         dma((n - 1,)), dma((n - 1,)),
@@ -423,26 +887,13 @@
         dma((n - 1, pieces)), dma((n - 1, pieces)),
         pltpu.VMEM((1, tok, kw), BF),
     ]
-    if scatter:
-        chunks = col_chunks(cols)
-        for _, w, _ in chunks:
-            scratch += [
-                pltpu.VMEM((kw // 2, w), BF), pltpu.VMEM((kw // 2, w), BF),
-                pltpu.VMEM((4, share, w), F32),
-                pltpu.VMEM((2, share, w), BF), pltpu.VMEM((2, share, w), BF),
-                pltpu.VMEM((share, w), BF), pltpu.VMEM((share, w), BF),
-            ]
-        scratch += [dma((len(chunks), 3)), dma((len(chunks), 3))]
     vmem = pl.BlockSpec(memory_space=pltpu.VMEM)
     anywhere = pl.BlockSpec(memory_space=pl.ANY)
     grad_keys, weight = pl.pallas_call(
         functools.partial(body, cfg),
         out_shape=(
-            pltpu.VMEM((1, kw, tok), BF),
-            pltpu.VMEM((share if scatter else kw, cols), F32),
-        ) if scatter else (
             jax.ShapeDtypeStruct((1, kw, tok), BF),
-            jax.ShapeDtypeStruct((share if scatter else kw, cols), F32),
+            jax.ShapeDtypeStruct((kw, cols), F32),
         ),
         in_specs=[vmem, vmem, vmem, anywhere, anywhere, anywhere],
         out_specs=(vmem, vmem),
@@ -450,8 +901,7 @@
         compiler_params=pltpu.CompilerParams(
             collective_id=0, has_side_effects=True, vmem_limit_bytes=60 * 1024 * 1024),
     )(jnp.swapaxes(latent, 1, 2), doc_ids, clip_limits, queries, out_grad, hidden)
-    if not scatter:
-        weight = lax.psum_scatter(weight, "grp", scatter_dimension=0, tiled=True)
+    weight = lax.psum_scatter(weight, "grp", scatter_dimension=0, tiled=True)
     return (jnp.swapaxes(grad_keys, 1, 2), weight)
 
 

time: 51.4 us -> 40.4 us (0.79)
  Pallas kernels: 49.1 us -> 38.1 us
    pallas_call x1, Pallas kernels: 49.1 us -> 38.1 us  [pair_call(): pl.pallas_call(functools.partial(pair_body, cfg), out_shape=(pltpu.VMEM((...]
where the time goes in v2:
time: 40.4 us; the launch traced here: 40.2 us
  Pallas kernels  38.1 us (94%)
  local copies, waits for them, and re-layouts  1.45 us (4%)
  between operations  0.64 us (2%)
    pallas_call x1, Pallas kernels, pair_call(): pl.pallas_call(functools.partial(pair_body, cfg), out_shape=(pltpu.VMEM((...  38.1 us
    unnamed x2, local copies, waits for them, and re-layouts  1.45 us

profile of v2, /device:TPU:0, one launch (start us, length us, event | category | flops | bytes accessed | tf_op | source)
XLA Modules:
  0.0 40.2 jit_solution(13924307650803811302)
XLA Ops:
  0.6 38.1 %shard_map.77 = (bf16[1,576,128]{2,1,0:T(8,128)(2,1)S(1)}, f32[72,1792]{1,0:T(8,128)S(1)}) custom-call(bf16[1,576,128]{2,1,0:T(8,128)(2,1)} %bitcast.3, s32[1,128]{1,0:T(1,128)} %refs_1_.1, f32[1,8]{1,0:T(1,128)} %refs_2_.1, bf16[1,4,73728]{2,1,0:T(4,128)(2,1)} %refs_3_.1, bf16[1,4,65536]{2,1,0:T(4,128)(2,1)} %refs_4_.1, bf16[1,512,1792]{2,1,0:T(8,128)(2,1)} %refs_5_.1), custom_call_target="tpu_custom_call" | custom-call | tf_op jit(solution)/shard_map/pallas_call | solution.py:832
  38.8 0.7 %copy.10 = bf16[1,128,576]{1,2,0:T(8,128)(2,1)} copy(bf16[1,128,576]{1,2,0:T(8,128)(2,1)S(1)} %bitcast.2) | data formatting | bytes 294912
  39.4 0.8 %copy.11 = f32[72,1792]{1,0:T(8,128)} copy(f32[72,1792]{1,0:T(8,128)S(1)} %get-tuple-element.7) | data formatting | bytes 1032192

commit v3 on v2

--- a/solution.py
+++ b/solution.py
@@ -307,12 +307,11 @@
     share = kw // 8
     np_ = len(splits)
     offs = [sum(splits[:p]) for p in range(np_)]
-    (lat_hbm, ids_hbm, lim_hbm, q_hbm, g_hbm, h_hbm, gk_out, w_out,
-     lat_t, lat, ids, lim, qraw, graw, hid, qs, gs, kbuf, krot, kgot, lath, hkey, idbuf,
+    (lat_hbm, ids_hbm, lim_hbm, q_hbm, g_hbm, h_hbm, gk_dst, w_dst,
+     gk_out, w_out, lat_t, lat, ids, lim, qraw, graw, hid, qs, gs, kbuf, krot, kgot, lath, hkey, idbuf,
      psend, precv, hsend, hrecv, ownb, own2, full, gkr, nbuf, lhs,
-     loc, id_s, id_r, key_s, key_r, hid_s, hid_r, part_s, part_r, halo_s, halo_r,
-     own_s, own_r, gk_s, gk_r, nrm_s, nrm_r, blk_s, blk_r, rs_s, rs_r) = refs[:54]
-    tail = refs[54:]
+     loc, out_s, key_r, hid_r, part_r, halo_r, own_r, gk_r, nrm_r, blk_r, rs_r) = refs[:46]
+    tail = refs[46:]
     d = lax.axis_index("ctx")
     m = lax.axis_index("grp")
     c = lax.rem(m, 2)
@@ -322,6 +321,7 @@
     mate = base + 1 - c
     flip_x = m + 2 - 4 * xb
     flip_y = m + 4 - 8 * yb
+    flip_xy = flip_x + flip_y - m
     cols = w_out.shape[1]
     wing = cols // 2
 
@@ -330,6 +330,9 @@
             src_ref=src, dst_ref=dst, send_sem=ss, recv_sem=rs,
             device_id=where, device_id_type=pl.DeviceIdType.MESH,
         )
+
+    def drain(ref, sem):
+        pltpu.make_async_copy(ref, ref, sem).wait()
 
     loads = [
         pltpu.make_async_copy(lat_hbm, lat_t, loc.at[0]),
@@ -347,12 +350,19 @@
     def greet(**where):
         pl.semaphore_signal(barrier, inc=1, device_id=where, device_id_type=pl.DeviceIdType.MESH)
 
-    for o in range(n):
-        if o:
-            greet(ctx=lax.rem(d + o, n), grp=m)
-        greet(ctx=lax.rem(d + o, n), grp=mate)
+    close = 0
+    for o in (-2, 2, -1, 1):
+        there = (d + o >= 0) & (d + o < n)
+        close = close + jnp.where(there, 2, 0)
+
+        @pl.when(there)
+        def _(o=o):
+            for who in (m, mate):
+                greet(ctx=jnp.clip(d + o, 0, n - 1), grp=who)
+    greet(grp=mate)
     greet(grp=flip_x)
     greet(grp=flip_y)
+    greet(grp=flip_xy)
 
     loads[0].wait()
     keys_t = jnp.concatenate([lat_t[0].astype(F32), jnp.zeros((pad, tok), F32)], axis=0)
@@ -363,19 +373,19 @@
     krot[...] = jnp.concatenate([keys[:near, LATENT:kw], keys[near:, LATENT:kw]], axis=1).astype(BF)
     lath[...] = keys[tok - halo:].astype(BF)
     loads[1].wait()
-    pl.semaphore_wait(barrier, 2 * n + 1)
+    pl.semaphore_wait(barrier, close + 4)
 
     def id_copy(k):
-        return remote(ids, idbuf.at[k - 1], id_s.at[k - 1], id_r.at[k - 1], ctx=lax.rem(d + k, n))
+        return remote(ids, idbuf.at[k - 1], out_s.at[12 + k], key_r.at[k - 1], ctx=lax.rem(d + k, n))
 
     def key_copy(k):
         if k == 1:
             return [
                 remote(lat.at[:, pl.ds(0, LATENT)], kbuf.at[pl.ds(0, tok), pl.ds(0, LATENT)],
-                       key_s.at[0], key_r.at[0], ctx=lax.rem(d + 1, n)),
-                remote(krot, kgot, key_s.at[2], key_r.at[2], ctx=lax.rem(d + 1, n)),
+                       out_s.at[15], key_r.at[2], ctx=lax.rem(d + 1, n)),
+                remote(krot, kgot, out_s.at[16], key_r.at[3], ctx=lax.rem(d + 1, n)),
             ]
-        return [remote(lath, hkey, key_s.at[1], key_r.at[1], ctx=lax.rem(d + 2, n))]
+        return [remote(lath, hkey, out_s.at[17], key_r.at[4], ctx=lax.rem(d + 2, n))]
 
     for k in (2, 1):
         @pl.when(d + k < n)
@@ -384,7 +394,7 @@
             for copy in key_copy(k):
                 copy.start()
 
-    hid_copy = remote(h_hbm.at[0], hid.at[c], hid_s.at[0], hid_r.at[0], grp=mate)
+    hid_copy = remote(h_hbm.at[0], hid.at[c], out_s.at[0], hid_r.at[0], grp=mate)
     hid_copy.start()
 
     @pl.when(d < 1)
@@ -483,12 +493,12 @@
         return out
 
     def halo_copy(h):
-        return remote(hsend, hrecv.at[c], halo_s.at[h], halo_r.at[c],
+        return remote(hsend, hrecv.at[c], out_s.at[2], halo_r.at[0],
                       ctx=jnp.maximum(d - 2, 0), grp=base + h)
 
     def part_copy(h, p):
         rows = pl.ds(4 * offs[p], 4 * splits[p])
-        return remote(psend.at[h, rows], precv.at[c, rows], part_s.at[h, p], part_r.at[c, p],
+        return remote(psend.at[h, rows], precv.at[c, rows], out_s.at[1], part_r.at[p],
                       ctx=jnp.maximum(d - 1, 0), grp=base + h)
 
     part1 = part_of(w1, dp1)
@@ -520,7 +530,7 @@
     turned = halves(jnp.transpose(part_of(w0, dp0)))
     for h in (0, 1):
         ownb[h] = turned[h].astype(BF)
-    own_copy = remote(ownb.at[1 - c], own2.at[c], own_s.at[0], own_r.at[0], grp=mate)
+    own_copy = remote(ownb.at[1 - c], own2.at[c], out_s.at[3], own_r.at[0], grp=mate)
     own_copy.start()
     own2[c] = ownb[c]
     own_copy.wait_recv()
@@ -530,44 +540,35 @@
 
     steps = (-1, 1, -2, 2)
 
+    def slot(o, source):
+        if o in (-1, 1):
+            return 1
+        return jnp.where(source == (n - 1 if o < 0 else 0), 0, 1)
+
     def spread(o, p):
-        i = steps.index(o)
         ref = full.at[d, rows_at(p)]
-        return remote(ref, ref, blk_s.at[i, p], blk_r.at[i, p], ctx=jnp.clip(d + o, 0, n - 1))
+        return remote(ref, ref, out_s.at[7 + steps.index(o)], blk_r.at[slot(o, d), p], ctx=jnp.clip(d + o, 0, n - 1))
 
     def spread_from(o, p):
-        i = steps.index(o)
         ref = full.at[jnp.clip(d - o, 0, n - 1), rows_at(p)]
-        return remote(ref, ref, blk_s.at[i, p], blk_r.at[i, p], ctx=jnp.clip(d - o, 0, n - 1))
+        return remote(ref, ref, out_s.at[7 + steps.index(o)], blk_r.at[slot(o, d - o), p], ctx=jnp.clip(d - o, 0, n - 1))
 
     def pass_end(o, p):
-        i = 4 if o < 0 else 5
         ref = full.at[n - 1 if o < 0 else 0, rows_at(p)]
-        return remote(ref, ref, blk_s.at[i, p], blk_r.at[i, p], ctx=jnp.clip(d + o, 0, n - 1))
+        return remote(ref, ref, out_s.at[11 if o < 0 else 12], blk_r.at[1, p], ctx=jnp.clip(d + o, 0, n - 1))
 
     def reaches(o):
         return (d + o >= 0) & (d + o < n)
 
-    def comes(o):
-        return (d - o >= 0) & (d - o < n)
-
     def passes(o):
         return d == (1 if o < 0 else n - 2)
 
     def ends(o):
         return d == (0 if o < 0 else n - 1)
 
-    def halo_from(g):
-        return remote(hsend, hrecv.at[g], halo_s.at[0], halo_r.at[g], grp=mate)
-
-    def part_from(g, p):
-        rows = pl.ds(4 * offs[p], 4 * splits[p])
-        return remote(psend.at[0, rows], precv.at[g, rows], part_s.at[0, p], part_r.at[g, p], grp=mate)
-
     @pl.when(d + 2 < n)
     def _():
-        for g in (0, 1):
-            halo_from(g).wait_recv()
+        drain(hrecv, halo_r.at[0])
 
     side = []
     for g in (0, 1):
@@ -585,8 +586,7 @@
     for p in range(np_):
         @pl.when(d + 1 < n)
         def _(p=p):
-            for g in (0, 1):
-                part_from(g, p).wait_recv()
+            drain(precv.at[:, pl.ds(4 * offs[p], 4 * splits[p])], part_r.at[p])
         lo, size = 4 * offs[p], 4 * splits[p]
         for g in (0, 1):
             value = own2[g, lo:lo + size].astype(F32) + precv[g, lo:lo + size].astype(F32)
@@ -603,25 +603,33 @@
         token_norm + [own_ids.astype(F32), limits, jnp.zeros((4, tok), F32)], axis=0)
 
     def norm_copy(o, flip):
-        i = 2 * o + flip - 1
         ref = nbuf.at[c, d]
-        return remote(ref, ref, nrm_s.at[i], nrm_r.at[i], ctx=lax.rem(d + o, n), grp=mate if flip else m)
-
-    def norm_from(o, flip):
-        i = 2 * o + flip - 1
-        ref = nbuf.at[1 - c if flip else c, lax.rem(d - o + n, n)]
-        return remote(ref, ref, nrm_s.at[i], nrm_r.at[i], ctx=lax.rem(d + o, n), grp=mate if flip else m)
+        return remote(ref, ref, out_s.at[5 + flip], nrm_r.at[flip], ctx=lax.rem(d + o, n), grp=mate if flip else m)
 
     peers = [(o, flip) for o in range(n) for flip in (0, 1) if o or flip]
     for o, flip in peers:
         norm_copy(o, flip).start()
-    for p in range(1, np_):
-        spread_all(p)
+    spread_all(1)
+
+    def spread_rest(p):
+        if p < np_:
+            @pl.when(ends(-1) | ends(1))
+            def _():
+                spread_all(p)
+
+    def spread_mid(p):
+        if p < np_:
+            @pl.when(jnp.logical_not(ends(-1) | ends(1)))
+            def _():
+                spread_all(p)
+
+    for p in range(2, np_):
+        spread_rest(p)
 
     def gk_copy(p):
         lo, size = 4 * offs[p], 4 * splits[p]
         src = full.at[d, pl.ds(pl.multiple_of(2 * lo + (1 - c) * size, 16), size)]
-        return remote(src, gkr.at[pl.ds(lo, size)], gk_s.at[p], gk_r.at[p], grp=mate)
+        return remote(src, gkr.at[pl.ds(lo, size)], out_s.at[4], gk_r.at[0], grp=mate)
 
     for p in range(np_):
         gk_copy(p).start()
@@ -629,8 +637,8 @@
     factors = []
 
     def make_factors():
-        for o, flip in peers:
-            norm_from(o, flip).wait_recv()
+        drain(nbuf.at[0, pl.ds(0, n - 1)], nrm_r.at[0])
+        drain(nbuf.at[0], nrm_r.at[1])
         rows = -(-ndocs // 8) * 8
         sub = lax.broadcasted_iota(jnp.int32, (rows, tok), 0).astype(F32)
         lane = lax.broadcasted_iota(jnp.int32, (rows, tok), 1).astype(F32)
@@ -649,31 +657,49 @@
             def _(o=o):
                 spread_from(2 * o, p).wait_recv()
                 pass_end(o, p).start()
+        spread_mid(p + 2)
 
     def gather(p):
-        for o in steps:
-            keep = comes(o)
-            if o in (-2, 2):
-                keep = keep & jnp.logical_not(passes(o // 2))
-
-            @pl.when(keep)
-            def _(o=o):
-                spread_from(o, p).wait_recv()
-        for o in (-1, 1):
-            @pl.when(ends(o))
-            def _(o=o):
-                pass_end(o, p).wait_recv()
-
-    bufs = [[tail[5 * (2 * p + w):5 * (2 * p + w) + 5] for w in (0, 1)] for p in range(np_)]
+        @pl.when(ends(-1) | ends(1))
+        def _():
+            drain(full.at[pl.ds(0, n - 1), rows_at(p)], blk_r.at[1, p])
+
+        @pl.when(jnp.logical_not(ends(-1) | ends(1)))
+        def _():
+            drain(full.at[pl.ds(0, n - 2), rows_at(p)], blk_r.at[1, p])
+
+    straight = cfg["straight"]
+    bufs, pos = [], 0
+    for p in range(np_):
+        if p in straight:
+            bufs.append(tail[pos:pos + 3])
+            pos += 3
+        else:
+            bufs.append(tail[pos:pos + 3])
+            pos += 3
+
+    def direct(p, j):
+        out, back, _ = bufs[p]
+        return remote(out.at[j], back.at[j], out_s.at[18 + p], rs_r.at[p, 0, 0],
+                      grp=(flip_x, flip_y, flip_xy)[j])
 
     def hop(p, w, stage):
-        first, back, second, back2, _ = bufs[p][w]
+        out, back, _ = bufs[p]
         where = (flip_x, flip_y) if w == 0 else (flip_y, flip_x)
-        src, dst = (first, back) if stage == 0 else (second, back2)
-        return remote(src, dst, rs_s.at[p, w, stage], rs_r.at[p, w, stage], grp=where[stage])
+        part = pl.ds(0, 2) if stage == 0 else pl.ds(2, 1)
+        src, dst = out.at[w, part], back.at[w, part]
+        return remote(src, dst, out_s.at[18 + p], rs_r.at[p, w, stage], grp=where[stage])
+
+    bits = ((xb, yb), (yb, xb))
 
     def chip(w, moving, other):
         return other * 2 + moving if w == 0 else moving * 2 + other
+
+    def wing_of(p, w):
+        lo, size = 4 * offs[p], 4 * splits[p]
+        return sum(
+            dot(lhs[lo:lo + size, g * seq:(g + 1) * seq], hid[g, :, w * wing:(w + 1) * wing], ((1,), (0,)))
+            for g in (0, 1))
 
     def product(p):
         lo, size = 4 * offs[p], 4 * splits[p]
@@ -682,36 +708,56 @@
                 value = full[b, 2 * lo + g * size:2 * lo + (g + 1) * size].astype(F32)
                 at = (g * n + b) * tok
                 lhs[lo:lo + size, at:at + tok] = (value * factors[g][b]).astype(BF)
+        if p in straight:
+            first, _, total = bufs[p]
+            for w in (0, 1):
+                cut = slice(w * wing, (w + 1) * wing)
+                total[:, :, cut] = wing_of(p, w).reshape(4, splits[p], wing)
+            for j, q in ((2, 2 * (1 - yb) + 1 - xb), (0, 2 * yb + 1 - xb), (1, 2 * (1 - yb) + xb)):
+                first[j] = total[q].astype(BF)
+                direct(p, j).start()
+            return
         for w in (0, 1):
-            first, _, _, _, total = bufs[p][w]
-            out = sum(
-                dot(lhs[lo:lo + size, g * seq:(g + 1) * seq], hid[g, :, w * wing:(w + 1) * wing], ((1,), (0,)))
-                for g in (0, 1))
-            total[...] = out.reshape(total.shape)
-            mb = xb if w == 0 else yb
+            first, _, total = bufs[p]
+            total[w] = wing_of(p, w).reshape(total.shape[1:])
             for o in (0, 1):
-                first[o] = total[chip(w, 1 - mb, o)].astype(BF)
+                first[w, o] = total[w, chip(w, 1 - bits[w][0], o)].astype(BF)
             hop(p, w, 0).start()
 
     def pass_on(p):
         for w in (0, 1):
-            _, back, second, _, total = bufs[p][w]
-            mb, ob = (xb, yb) if w == 0 else (yb, xb)
+            second, back, total = bufs[p]
             hop(p, w, 0).wait_recv()
-            second[...] = (total[chip(w, mb, 1 - ob)] + back[1 - ob].astype(F32)).astype(BF)
+            second[w, 2] = (total[w, chip(w, bits[w][0], 1 - bits[w][1])] + back[w, 1 - bits[w][1]].astype(F32)).astype(BF)
             hop(p, w, 1).start()
 
+    def put(p):
+        rows = pl.ds(offs[p], splits[p])
+        return pltpu.make_async_copy(w_out.at[rows], w_dst.at[rows], loc.at[7])
+
+    put_keys = pltpu.make_async_copy(gk_out, gk_dst, loc.at[6])
+
+    def finish(p):
+        last(p)
+        put(p).start()
+
     def last(p):
+        if p in straight:
+            _, back, total = bufs[p]
+            value = total[2 * yb + xb]
+            drain(back, rs_r.at[p, 0, 0])
+            for j in range(3):
+                value = value + back[j].astype(F32)
+            w_out[offs[p]:offs[p] + splits[p], :] = value
+            return
         for w in (0, 1):
-            _, back, _, back2, total = bufs[p][w]
-            mb, ob = (xb, yb) if w == 0 else (yb, xb)
-            kept = total[chip(w, mb, ob)] + back[ob].astype(F32)
+            _, back, total = bufs[p]
+            kept = total[w, chip(w, bits[w][0], bits[w][1])] + back[w, bits[w][1]].astype(F32)
             hop(p, w, 1).wait_recv()
-            w_out[offs[p]:offs[p] + splits[p], w * wing:(w + 1) * wing] = kept + back2[...].astype(F32)
+            w_out[offs[p]:offs[p] + splits[p], w * wing:(w + 1) * wing] = kept + back[w, 2].astype(F32)
 
     def write_keys():
-        for p in range(np_):
-            gk_copy(p).wait_recv()
+        drain(gkr, gk_r.at[0])
         order = [None] * (8 * np_)
         for p in range(np_):
             lo, size = 4 * offs[p], splits[p]
@@ -723,11 +769,14 @@
                 for q in range(4):
                     order[(2 * q + h) * np_ + p] = value[q * size:(q + 1) * size]
         gk_out[0] = jnp.concatenate(order, axis=0).astype(BF)
+        put_keys.start()
 
     forward(0)
     make_factors()
     loads[5].wait()
     hid_copy.wait_recv()
+    staged = [p for p in range(np_) if p not in straight]
+    moved, done = [], []
     for p in range(np_):
         if p + 1 < np_:
             forward(p + 1)
@@ -735,14 +784,21 @@
         product(p)
         if p == 0:
             write_keys()
-        if p >= 1:
-            pass_on(p - 1)
-        if p >= 2:
-            last(p - 2)
-    pass_on(np_ - 1)
-    if np_ >= 2:
-        last(np_ - 2)
-    last(np_ - 1)
+        for q in staged:
+            if q + cfg["lag"] == p:
+                pass_on(q)
+                moved.append(q)
+            if q + 2 * cfg["lag"] == p:
+                finish(q)
+                done.append(q)
+    for q in staged:
+        if q not in moved:
+            pass_on(q)
+    for q in range(np_):
+        if q not in done:
+            finish(q)
+    put_keys.wait()
+    drain(w_out, loc.at[7])
 
     for k in (1, 2):
         @pl.when(d + k < n)
@@ -754,32 +810,25 @@
 
     @pl.when(d >= 2)
     def _():
-        for h in (0, 1):
-            halo_copy(h).wait_send()
+        drain(hrecv, out_s.at[2])
 
     @pl.when(d >= 1)
     def _():
-        for p in range(np_):
-            for h in (0, 1):
-                part_copy(h, p).wait_send()
+        drain(psend, out_s.at[1])
     own_copy.wait_send()
+    drain(gkr, out_s.at[4])
+    drain(nbuf.at[0, pl.ds(0, n - 1)], out_s.at[5])
+    drain(nbuf.at[0], out_s.at[6])
+    for i, o in enumerate(steps):
+        @pl.when(reaches(o))
+        def _(i=i):
+            drain(full.at[0], out_s.at[7 + i])
+    for i, o in enumerate((-1, 1)):
+        @pl.when(passes(o))
+        def _(i=i):
+            drain(full.at[0], out_s.at[11 + i])
     for p in range(np_):
-        gk_copy(p).wait_send()
-    for o, flip in peers:
-        norm_copy(o, flip).wait_send()
-    for p in range(np_):
-        for o in steps:
-            @pl.when(reaches(o))
-            def _(p=p, o=o):
-                spread(o, p).wait_send()
-        for o in (-1, 1):
-            @pl.when(passes(o))
-            def _(p=p, o=o):
-                pass_end(o, p).wait_send()
-    for p in range(np_):
-        for w in (0, 1):
-            for stage in (0, 1):
-                hop(p, w, stage).wait_send()
+        drain(bufs[p][0], out_s.at[18 + p])
 
 
 def pair_scratch(cfg, latent, queries, out_grad, hidden, clip_limits):
@@ -794,6 +843,7 @@
     dma = pltpu.SemaphoreType.DMA
     v = pltpu.VMEM
     scratch = [
+        v((1, kw, tok), BF), v((kw // 8, cols), F32),
         v((1, kw, tok), BF), v((tok, wide), BF), v((1, tok), jnp.int32), v(clip_limits.shape, F32),
         v(queries.shape, BF), v(out_grad.shape, BF), v((2, seq, cols), BF),
         v((2 * rows, wide), BF), v((2 * rows, LATENT), BF),
@@ -802,20 +852,16 @@
         v((2, half, tok), BF), v((2, half, tok), BF), v((halo, wide), BF), v((2, halo, wide), BF),
         v((2, half, tok), BF), v((2, half, tok), BF), v((n, kw, tok), BF), v((half, tok), BF),
         v((2, n, 8, tok), F32), v((half, 2 * seq), BF),
-        dma((6,)), dma((2,)), dma((2,)), dma((3,)), dma((3,)), dma((1,)), dma((1,)),
-        dma((2, np_)), dma((2, np_)), dma((2,)), dma((2,)),
-        dma((1,)), dma((1,)), dma((np_,)), dma((np_,)),
-        dma((2 * n,)), dma((2 * n,)),
-        dma((6, np_)), dma((6, np_)),
-        dma((np_, 2, 2)), dma((np_, 2, 2)),
+        dma((8,)), dma((18 + np_,)), dma((5,)), dma((1,)), dma((np_,)), dma((1,)), dma((1,)), dma((1,)), dma((2,)),
+        dma((2, np_)), dma((np_, 2, 2)),
     ]
-    for size in splits:
-        for _ in (0, 1):
-            scratch += [
-                v((2, size, cols // 2), BF), v((2, size, cols // 2), BF),
-                v((size, cols // 2), BF), v((size, cols // 2), BF),
-                v((4, size, cols // 2), F32),
-            ]
+    for p, size in enumerate(splits):
+        if p in cfg["straight"]:
+            scratch += [v((3, size, cols), BF), v((3, size, cols), BF), v((4, size, cols), F32)]
+            continue
+        scratch += [
+            v((2, 3, size, cols // 2), BF), v((2, 3, size, cols // 2), BF), v((2, 4, size, cols // 2), F32),
+        ]
     return scratch
 
 
@@ -827,7 +873,6 @@
 
 def pair_call(cfg, latent, queries, out_grad, hidden, doc_ids, clip_limits):
     anywhere = pl.BlockSpec(memory_space=pl.ANY)
-    vmem = pl.BlockSpec(memory_space=pltpu.VMEM)
     tok, kw = cfg["tok"], cfg["kw"]
     grad_keys, weight = pl.pallas_call(
         functools.partial(pair_body, cfg),
@@ -836,7 +881,7 @@
             pltpu.VMEM((kw // 8, hidden.shape[2]), F32),
         ),
         in_specs=[anywhere] * 6,
-        out_specs=(vmem, vmem),
+        out_specs=(anywhere, anywhere),
         scratch_shapes=pair_scratch(cfg, latent, queries, out_grad, hidden, clip_limits),
         compiler_params=pltpu.CompilerParams(
             collective_id=0, has_side_effects=True, vmem_limit_bytes=56 * 1024 * 1024),
@@ -860,7 +905,7 @@
     paired = (groups == 8 and n == 4 and reach == 3 and last <= tok and cols % 256 == 0 and kw % 64 == 0
               and tok % 128 == 0 and ndocs <= tok and span <= 2 * tok + 16 and 2 * (kw - LATENT) == 128)
     if paired:
-        cfg = dict(n=n, tok=tok, kw=kw, qd=qd, halo=-(-(span - 2 * tok) // 4) * 4, span=span, ndocs=ndocs, splits=row_splits(share))
+        cfg = dict(n=n, tok=tok, kw=kw, qd=qd, halo=-(-(span - 2 * tok) // 4) * 4, span=span, ndocs=ndocs, splits=row_splits(share), straight=(0,), lag=1)
         return pair_call(cfg, latent, queries, out_grad, hidden, doc_ids, clip_limits)
     pieces = 2
     cfg = dict(n=n, tok=tok, kw=kw, qd=qd, reach=reach, rows_of=rows_of, span=span, ndocs=ndocs,

time: 40.4 us -> 39.4 us (0.975)
  Pallas kernels: 38.1 us -> 37.1 us
    pallas_call x1, Pallas kernels: 38.1 us -> 37.1 us  [pair_call(): pl.pallas_call(functools.partial(pair_body, cfg), out_shape=(pltpu.VMEM((...]
where the time goes in v3:
time: 39.4 us; the launch traced here: 39.2 us
  Pallas kernels  37.1 us (94%)
  local copies, waits for them, and re-layouts  1.45 us (4%)
  between operations  0.64 us (2%)
    pallas_call x1, Pallas kernels, pair_call(): pl.pallas_call(functools.partial(pair_body, cfg), out_shape=(pltpu.VMEM((...  37.1 us
    unnamed x2, local copies, waits for them, and re-layouts  1.45 us

profile of v3, /device:TPU:0, one launch (start us, length us, event | category | flops | bytes accessed | tf_op | source)
XLA Modules:
  0.0 39.2 jit_solution(10771393701660735556)
XLA Ops:
  0.6 37.1 %shard_map.77 = (bf16[1,576,128]{2,1,0:T(8,128)(2,1)S(1)}, f32[72,1792]{1,0:T(8,128)S(1)}) custom-call(bf16[1,576,128]{2,1,0:T(8,128)(2,1)} %bitcast.3, s32[1,128]{1,0:T(1,128)} %refs_1_.1, f32[1,8]{1,0:T(1,128)} %refs_2_.1, bf16[1,4,73728]{2,1,0:T(4,128)(2,1)} %refs_3_.1, bf16[1,4,65536]{2,1,0:T(4,128)(2,1)} %refs_4_.1, bf16[1,512,1792]{2,1,0:T(8,128)(2,1)} %refs_5_.1), custom_call_target="tpu_custom_call" | custom-call | tf_op jit(solution)/shard_map/pallas_call | solution.py:877
  37.8 0.7 %copy.10 = bf16[1,128,576]{1,2,0:T(8,128)(2,1)} copy(bf16[1,128,576]{1,2,0:T(8,128)(2,1)S(1)} %bitcast.2) | data formatting | bytes 294912
  38.5 0.8 %copy.11 = f32[72,1792]{1,0:T(8,128)} copy(f32[72,1792]{1,0:T(8,128)S(1)} %get-tuple-element.7) | data formatting | bytes 1032192

commit v4 on v3

--- a/solution.py
+++ b/solution.py
@@ -657,7 +657,8 @@
             def _(o=o):
                 spread_from(2 * o, p).wait_recv()
                 pass_end(o, p).start()
-        spread_mid(p + 2)
+        if p:
+            spread_mid(p + 1)
 
     def gather(p):
         @pl.when(ends(-1) | ends(1))
@@ -772,16 +773,17 @@
         put_keys.start()
 
     forward(0)
+    forward(1)
     make_factors()
     loads[5].wait()
     hid_copy.wait_recv()
     staged = [p for p in range(np_) if p not in straight]
     moved, done = [], []
     for p in range(np_):
-        if p + 1 < np_:
-            forward(p + 1)
         gather(p)
         product(p)
+        if p + 2 < np_:
+            forward(p + 2)
         if p == 0:
             write_keys()
         for q in staged:

time: 39.4 us -> 39.5 us (level)
  no operation moved by 1% of the time
where the time goes in v4:
time: 39.5 us; the launch traced here: 39.3 us
  Pallas kernels  37.2 us (94%)
  local copies, waits for them, and re-layouts  1.45 us (4%)
  between operations  0.64 us (2%)
    pallas_call x1, Pallas kernels, pair_call(): pl.pallas_call(functools.partial(pair_body, cfg), out_shape=(pltpu.VMEM((...  37.2 us
    unnamed x2, local copies, waits for them, and re-layouts  1.45 us

profile of v4, /device:TPU:0, one launch (start us, length us, event | category | flops | bytes accessed | tf_op | source)
XLA Modules:
  0.0 39.3 jit_solution(9769929895459409288)
XLA Ops:
  0.6 37.2 %shard_map.77 = (bf16[1,576,128]{2,1,0:T(8,128)(2,1)S(1)}, f32[72,1792]{1,0:T(8,128)S(1)}) custom-call(bf16[1,576,128]{2,1,0:T(8,128)(2,1)} %bitcast.3, s32[1,128]{1,0:T(1,128)} %refs_1_.1, f32[1,8]{1,0:T(1,128)} %refs_2_.1, bf16[1,4,73728]{2,1,0:T(4,128)(2,1)} %refs_3_.1, bf16[1,4,65536]{2,1,0:T(4,128)(2,1)} %refs_4_.1, bf16[1,512,1792]{2,1,0:T(8,128)(2,1)} %refs_5_.1), custom_call_target="tpu_custom_call" | custom-call | tf_op jit(solution)/shard_map/pallas_call | solution.py:879
  37.9 0.7 %copy.10 = bf16[1,128,576]{1,2,0:T(8,128)(2,1)} copy(bf16[1,128,576]{1,2,0:T(8,128)(2,1)S(1)} %bitcast.2) | data formatting | bytes 294912
  38.5 0.8 %copy.11 = f32[72,1792]{1,0:T(8,128)} copy(f32[72,1792]{1,0:T(8,128)S(1)} %get-tuple-element.7) | data formatting | bytes 1032192
